TPU v7x, 32 devices: a whole 2x2x4 slice. The times are simulated.
32 devices in a mesh: gx: 4 (over x, core), gy: 8 (over z, y).
Axes of the slice: x: 2, y: 2, z: 4, core: 2. Of those that a mesh axis runs over, the one named last changes fastest.
Arguments:
- right_side: float32 [2, 64, 256, 128], P(None, 'gx', 'gy'), may hold values from -6 to 6
- wavenumber: float32 [64, 256, 128], P('gx', 'gy'), may hold values from 0.2 to 1
- pml_layer: int32 [64, 256, 128], P('gx', 'gy'), may hold values from 0 to 3
- aggregate: int32 [64, 256, 128], P('gx', 'gy'), may hold values from 0 to 15, as said below
- coarse_inverse: float32 [2, 512, 512], P(None, ('gx', 'gy')), may hold values from -0.0029296875 to 0.0029296875
Outputs:
- solution: float32 [2, 64, 256, 128], P(None, 'gx', 'gy')
- hessenberg: float32 [2, 5, 4], replicated
Inputs may be any that keep to these rules, and one draw needn't show every extreme that they name: `aggregate`: along the third dimension the value never falls, and every value of 0 to 15 occurs in every column of cells.
All inputs are finite; a program needn't handle non-finite values.
Results may differ from a plain program's by a relative error of at most 0.00015.
Values sent between devices are 32-bit elements; how exact they have to be, the bound alone decides.
No kernel may reach another device: no remote copies, remote signals or barrier semaphores. Data moves between devices by JAX's collectives and lax.ppermute only.
A program may use at most 64 MiB of HBM per device.

v0:
```python
import math
import jax
import jax.numpy as jnp
from jax import lax
from jax.sharding import PartitionSpec as P

ITERS = 4
damping = 0.8
pml_strength = 3.0
epsilon = 1e-06


def with_halo(block, sides, width):
    for axis, dim in sides:
        count = lax.axis_size(axis)
        forward = [(i, i + 1) for i in range(count - 1)]
        backward = [(target, source) for source, target in forward]
        low = lax.ppermute(
            lax.slice_in_dim(block, block.shape[dim] - width, None, axis=dim), axis, forward
        )
        high = lax.ppermute(lax.slice_in_dim(block, 0, width, axis=dim), axis, backward)
        block = jnp.concatenate([low, block, high], axis=dim)
    return block


def coefficients(wavenumber, layer_float):
    wave_sq = wavenumber * wavenumber
    depth = layer_float / 3.0
    absorb = wave_sq * (pml_strength * depth * depth)
    diag_re = 6.0 - wave_sq
    magnitude = diag_re * diag_re + absorb * absorb
    return (wave_sq, absorb, damping * diag_re / magnitude, damping * absorb / magnitude)


def operate_inner(extended, wave_sq, absorb):
    middle = extended[:, 1:-1, 1:-1]
    above = jnp.concatenate([middle[..., 1:], jnp.zeros_like(middle[..., :1])], -1)
    below = jnp.concatenate([jnp.zeros_like(middle[..., :1]), middle[..., :-1]], -1)
    beside = (
        extended[:, 2:, 1:-1]
        + extended[:, :-2, 1:-1]
        + extended[:, 1:-1, 2:]
        + extended[:, 1:-1, :-2]
        + above
        + below
    )
    real_part = (6.0 - wave_sq) * middle[0] - beside[0] + absorb * middle[1]
    imag_part = (6.0 - wave_sq) * middle[1] - beside[1] - absorb * middle[0]
    return jnp.stack([real_part, imag_part])


def smooth(field, scale_re, scale_im):
    return jnp.stack(
        [scale_re * field[0] - scale_im * field[1], scale_re * field[1] + scale_im * field[0]]
    )


def complex_scale(scale_re, scale_im, field):
    return jnp.stack(
        [scale_re * field[0] - scale_im * field[1], scale_re * field[1] + scale_im * field[0]]
    )


def inner_local(left, right):
    return jnp.stack(
        [
            jnp.sum(left[0] * right[0] + left[1] * right[1]),
            jnp.sum(left[0] * right[1] - left[1] * right[0]),
        ]
    )


def least_squares(hessenberg, beta):
    real_h = hessenberg[0]
    imag_h = hessenberg[1]
    stacked = jnp.concatenate(
        [jnp.concatenate([real_h, -imag_h], 1), jnp.concatenate([imag_h, real_h], 1)], 0
    )
    count = stacked.shape[1]
    target = jnp.zeros((stacked.shape[0],), jnp.float32).at[0].set(beta)
    ortho = []
    upper = {}
    for column in range(count):
        vector = stacked[:, column]
        for position in range(column):
            upper[position, column] = jnp.zeros((), jnp.float32)
        for repeat in range(2):
            for position in range(len(ortho)):
                weight = jnp.sum(ortho[position] * vector)
                vector = vector - weight * ortho[position]
                upper[position, column] = upper[position, column] + weight
        norm_value = jnp.sqrt(jnp.sum(vector * vector))
        upper[column, column] = norm_value
        ortho.append(vector / norm_value)
    project = [jnp.sum(basis_vec * target) for basis_vec in ortho]
    solved = [None] * count
    for column in reversed(range(count)):
        total = project[column]
        for later in range(column + 1, count):
            total = total - upper[column, later] * solved[later]
        solved[column] = total / upper[column, column]
    return solved


def restrict(flat_field, flat_ids, levels_count):
    total = flat_ids.shape[0]
    block = math.gcd(total, 16384)
    levels = jnp.arange(levels_count, dtype=jnp.int32)

    def accumulate(step_index, result):
        piece = lax.dynamic_slice_in_dim(flat_field, step_index * block, block, 1)
        labels = lax.dynamic_slice_in_dim(flat_ids, step_index * block, block, 0)
        onehot = (labels[None, :] == levels[:, None]).astype(jnp.float32)
        return result + lax.dot_general(
            piece, onehot, (((1,), (1,)), ((), ())), precision=lax.Precision.HIGHEST
        )

    return lax.fori_loop(0, total // block, accumulate, jnp.zeros((2, levels_count), jnp.float32))


def prolong(values, flat_ids):
    total = flat_ids.shape[0]
    block = math.gcd(total, 16384)
    levels = jnp.arange(values.shape[1], dtype=jnp.int32)

    def place(step_index, result):
        labels = lax.dynamic_slice_in_dim(flat_ids, step_index * block, block, 0)
        onehot = (levels[:, None] == labels[None, :]).astype(jnp.float32)
        piece = jnp.dot(values, onehot, precision=lax.Precision.HIGHEST)
        return lax.dynamic_update_slice_in_dim(result, piece, step_index * block, 1)

    return lax.fori_loop(0, total // block, place, jnp.zeros((2, total), jnp.float32))


def coarse_fix(remainder, flat_ids, coarse_inverse):
    highest = lax.Precision.HIGHEST
    levels_count = coarse_inverse.shape[1]
    total_coarse = coarse_inverse.shape[2]
    partial_value = restrict(remainder.reshape(2, -1), flat_ids, levels_count)
    offset = (lax.axis_index("gx") * lax.axis_size("gy") + lax.axis_index("gy")) * levels_count
    padded = lax.dynamic_update_slice(
        jnp.zeros((2, total_coarse), jnp.float32), partial_value, (jnp.zeros((), jnp.int32), offset)
    )
    whole = lax.psum(padded, ("gx", "gy"))
    own_re = jnp.dot(coarse_inverse[0], whole[0], precision=highest) - jnp.dot(
        coarse_inverse[1], whole[1], precision=highest
    )
    own_im = jnp.dot(coarse_inverse[0], whole[1], precision=highest) + jnp.dot(
        coarse_inverse[1], whole[0], precision=highest
    )
    return prolong(jnp.stack([own_re, own_im]), flat_ids).reshape(remainder.shape)


def operate_near(field, wave_sq, absorb):
    extended = with_halo(field, (("gx", 1), ("gy", 2)), 1)
    return operate_inner(extended, wave_sq, absorb)


def operate_final(field, wave_sq, absorb):
    extended = with_halo(field, (("gx", 1), ("gy", 2)), 1)
    return operate_inner(extended, wave_sq, absorb)


def body(right_side, wavenumber, pml_layer, aggregate, coarse_inverse):
    layer_float = pml_layer.astype(jnp.float32)
    wave_sq, absorb, scale_re, scale_im = coefficients(wavenumber, layer_float)
    flat_ids = aggregate.reshape(-1)
    beta = jnp.sqrt(lax.psum(jnp.sum(right_side * right_side), ("gx", "gy")) + epsilon)
    basis = [right_side / beta]
    directions = []
    columns_re = []
    columns_im = []
    for column in range(ITERS):
        vector = basis[column]
        first = smooth(vector, scale_re, scale_im)
        second = first + smooth(vector - operate_near(first, wave_sq, absorb), scale_re, scale_im)
        remainder = vector - operate_near(second, wave_sq, absorb)
        direction = second + coarse_fix(remainder, flat_ids, coarse_inverse)
        image = operate_final(direction, wave_sq, absorb)
        local_dots = jnp.stack([inner_local(member, image) for member in basis], 1)
        dots, squared = lax.psum((local_dots, jnp.sum(image * image)), ("gx", "gy"))
        for position in range(len(basis)):
            image = image - complex_scale(dots[0, position], dots[1, position], basis[position])
        leftover = squared - jnp.sum(dots * dots)
        length = jnp.sqrt(jnp.maximum(leftover, 0.0) + epsilon)
        tail = jnp.zeros((ITERS - 1 - column,), jnp.float32)
        columns_re.append(jnp.concatenate([dots[0], length[None], tail]))
        columns_im.append(jnp.concatenate([dots[1], jnp.zeros((1,), jnp.float32), tail]))
        directions.append(direction)
        if column + 1 < ITERS:
            basis.append(image / length)
    hessenberg = jnp.stack([jnp.stack(columns_re, 1), jnp.stack(columns_im, 1)])
    solved = least_squares(hessenberg, beta)
    solution = jnp.zeros_like(right_side)
    for column in range(ITERS):
        solution = solution + complex_scale(
            solved[column], solved[ITERS + column], directions[column]
        )
    return (solution, hessenberg)


def solution(mesh):
    return jax.shard_map(
        body,
        mesh=mesh,
        in_specs=(
            P(None, "gx", "gy", None),
            P("gx", "gy", None),
            P("gx", "gy", None),
            P("gx", "gy", None),
            P(None, ("gx", "gy"), None),
        ),
        out_specs=(P(None, "gx", "gy", None), P()),
        check_vma=False,
    )
```

profile of v0, /device:TPU:0, one launch (start us, length us, event | category | flops | bytes accessed | tf_op | source)
XLA Modules:
  0.0 809.6 jit_solution(285482413600228902)
XLA Ops:
  2.5 42.2 %psum.91 = f32[]{:T(128)} all-reduce(f32[]{:T(128)} %multiply_reduce_fusion.3), channel_id=1, replica_groups=mesh['gx'=4,'gy'=8] {'gx','gy'}, use_global_device_ids=true, to_apply=%region_1.0 | all-reduce | flops 1 | bytes 8 | tf_op jit(solution)/shard_map/psum | solution.py:168
  48.0 3.0 collective-permute-start.1
  53.2 5.0 collective-permute-start.3
  62.3 3.0 collective-permute-start.5
  67.5 5.4 collective-permute-start.7
  76.2 7.0 while.117
  83.3 46.5 %psum.92 = f32[2,512]{1,0:T(2,128)S(1)} all-reduce(f32[2,512]{1,0:T(2,128)S(1)} %dynamic_update_slice.40), channel_id=1, replica_groups=mesh['gx'=4,'gy'=8] {'gx','gy'}, use_global_device_ids=true, to_apply=%region_4.0 | all-reduce | flops 1024 | bytes 8192 | tf_op jit(solution)/shard_map/psum | solution.py:144
  134.9 3.0 collective-permute-start.9
  140.2 4.8 collective-permute-start.11
  149.7 43.8 %all-reduce.29 = (f32[2,1]{0,1:T(1,128)S(1)}, f32[]{:T(128)}) all-reduce(f32[2,1]{0,1:T(1,128)S(1)} %maximum_bitcast_fusion.1, f32[]{:T(128)} %multiply_reduce_fusion.2), channel_id=1, replica_groups=mesh['gx'=4,'gy'=8] {'gx','gy'}, use_global_device_ids=true, to_apply=%region_9.0 | all-reduce | flops 3 | bytes 24 | tf_op jit(solution)/shard_map/psum | solution.py:181
  199.2 3.0 collective-permute-start.13
  204.4 5.0 collective-permute-start.15
  214.4 3.4 collective-permute-start.17
  220.2 5.6 collective-permute-start.19
  228.3 2.1 divide_subtract_fusion.2
  230.3 6.9 while.118
  237.5 47.6 %psum.95 = f32[2,512]{1,0:T(2,128)S(1)} all-reduce(f32[2,512]{1,0:T(2,128)S(1)} %dynamic_update_slice.41), channel_id=1, replica_groups=mesh['gx'=4,'gy'=8] {'gx','gy'}, use_global_device_ids=true, to_apply=%region_15.0 | all-reduce | flops 1024 | bytes 8192 | tf_op jit(solution)/shard_map/psum | solution.py:144
  290.5 3.0 collective-permute-start.21
  295.7 4.8 collective-permute-start.23
  306.9 43.6 %all-reduce.28 = (f32[2,2]{0,1:T(2,128)S(1)}, f32[]{:T(128)}) all-reduce(f32[2,2]{0,1:T(2,128)S(1)} %pad_maximum_fusion.166, f32[]{:T(128)} %multiply_reduce_fusion.1), channel_id=1, replica_groups=mesh['gx'=4,'gy'=8] {'gx','gy'}, use_global_device_ids=true, to_apply=%region_22.0 | all-reduce | flops 5 | bytes 40 | tf_op jit(solution)/shard_map/psum | solution.py:181
  357.4 3.0 collective-permute-start.25
  362.6 5.0 collective-permute-start.27
  372.0 3.3 collective-permute-start.29
  377.5 5.3 collective-permute-start.31
  385.8 2.4 divide_subtract_fusion.1
  388.2 6.9 while.119
  395.3 47.6 %psum.98 = f32[2,512]{1,0:T(2,128)S(1)} all-reduce(f32[2,512]{1,0:T(2,128)S(1)} %dynamic_update_slice.42), channel_id=1, replica_groups=mesh['gx'=4,'gy'=8] {'gx','gy'}, use_global_device_ids=true, to_apply=%region_28.0 | all-reduce | flops 1024 | bytes 8192 | tf_op jit(solution)/shard_map/psum | solution.py:144
  448.4 3.0 collective-permute-start.33
  453.6 4.8 collective-permute-start.35
  467.3 43.7 %all-reduce.27 = (f32[2,3]{0,1:T(4,128)S(1)}, f32[]{:T(128)}) all-reduce(f32[2,3]{0,1:T(4,128)S(1)} %pad_maximum_fusion.161, f32[]{:T(128)} %multiply_reduce_fusion), channel_id=1, replica_groups=mesh['gx'=4,'gy'=8] {'gx','gy'}, use_global_device_ids=true, to_apply=%region_37.0 | all-reduce | flops 7 | bytes 56 | tf_op jit(solution)/shard_map/psum | solution.py:181
  513.7 2.5 multiply_subtract_fusion.5
  522.2 3.0 collective-permute-start.37
  528.0 5.1 collective-permute-start.39
  537.5 3.1 collective-permute-start.41
  542.8 5.5 collective-permute-start.43
  550.0 2.8 divide_subtract_fusion
  552.9 6.9 while.120
  560.0 47.0 %psum.101 = f32[2,512]{1,0:T(2,128)S(1)} all-reduce(f32[2,512]{1,0:T(2,128)S(1)} %dynamic_update_slice.43), channel_id=1, replica_groups=mesh['gx'=4,'gy'=8] {'gx','gy'}, use_global_device_ids=true, to_apply=%region_43.0 | all-reduce | flops 1024 | bytes 8192 | tf_op jit(solution)/shard_map/psum | solution.py:144
  608.5 4.3 while.116
  615.6 3.0 collective-permute-start.45
  620.8 4.8 collective-permute-start.47
  636.3 43.7 %all-reduce.26 = (f32[2,4]{0,1:T(4,128)S(1)}, f32[]{:T(128)}) all-reduce(f32[2,4]{0,1:T(4,128)S(1)} %pad_maximum_fusion.162, f32[]{:T(128)} %fusion.133), channel_id=1, replica_groups=mesh['gx'=4,'gy'=8] {'gx','gy'}, use_global_device_ids=true, to_apply=%region_54.0 | all-reduce | flops 9 | bytes 72 | tf_op jit(solution)/shard_map/psum | solution.py:181
  708.7 2.6 multiply_reduce_fusion.41
  715.1 2.6 multiply_reduce_fusion.39
  725.9 3.1 multiply_reduce_fusion.29
  736.5 2.6 multiply_reduce_fusion.19
  740.9 3.1 multiply_reduce_fusion.17
  749.0 2.6 multiply_reduce_fusion.15
  (490 shorter events, 229.7 us)
Async XLA Ops:
  46.7 4.3 collective-permute-start
  48.0 3.9 collective-permute-start.1
  51.9 6.5 collective-permute-start.2
  53.2 6.5 collective-permute-start.3
  61.0 4.3 collective-permute-start.4
  62.3 3.9 collective-permute-start.5
  66.2 7.0 collective-permute-start.6
  67.5 6.9 collective-permute-start.7
  133.6 4.3 collective-permute-start.8
  134.9 3.9 collective-permute-start.9
  138.9 6.3 collective-permute-start.10
  140.2 6.3 collective-permute-start.11
  197.9 4.3 collective-permute-start.12
  199.2 3.9 collective-permute-start.13
  203.1 6.5 collective-permute-start.14
  204.4 6.4 collective-permute-start.15
  213.1 4.7 collective-permute-start.16
  214.4 4.5 collective-permute-start.17
  218.9 7.1 collective-permute-start.18
  220.2 6.6 collective-permute-start.19
  289.2 4.3 collective-permute-start.20
  290.5 3.9 collective-permute-start.21
  294.4 6.3 collective-permute-start.22
  295.7 6.3 collective-permute-start.23
  356.1 4.3 collective-permute-start.24
  357.4 3.9 collective-permute-start.25
  361.3 6.5 collective-permute-start.26
  362.6 6.4 collective-permute-start.27
  370.7 4.6 collective-permute-start.28
  372.0 4.2 collective-permute-start.29
  376.2 6.9 collective-permute-start.30
  377.5 6.6 collective-permute-start.31
  447.1 4.4 collective-permute-start.32
  448.4 3.9 collective-permute-start.33
  452.3 6.3 collective-permute-start.34
  453.6 6.3 collective-permute-start.35
  520.9 5.8 collective-permute-start.36
  522.2 4.5 collective-permute-start.37
  526.7 6.6 collective-permute-start.38
  528.0 6.5 collective-permute-start.39
  536.2 4.6 collective-permute-start.40
  537.5 4.0 collective-permute-start.41
  541.5 7.1 collective-permute-start.42
  542.8 6.8 collective-permute-start.43
  614.3 4.4 collective-permute-start.44
  615.6 3.9 collective-permute-start.45
  619.5 6.3 collective-permute-start.46
  620.8 6.3 collective-permute-start.47
  (68 other events, 938.6 us)
where the time goes:
time: 821 us; the launch traced here: 810 us
  blocking collectives  406 us (49%)
  other arithmetic  135 us (16%)
  starting transfers between devices  129 us (16%)
  between operations  54.6 us (7%)
  matrix products  39.1 us (5%)
  waiting for transfers between devices  23 us (3%)
  local copies, waits for them, and re-layouts  22.3 us (3%)
    psum x4, blocking collectives, coarse_fix(): whole = lax.psum(padded, ('gx', 'gy'))  189 us
    psum x4, blocking collectives, body(): dots, squared = lax.psum((local_dots, jnp.sum(image * image)), ('gx', 'gy'))  175 us
    ppermute x24, starting transfers between devices, with_halo(): lax.ppermute(lax.slice_in_dim(block, block.shape[dim] - width, None, axis...  98.4 us
    reduce_sum x34, other arithmetic, least_squares(): weight = jnp.sum(ortho[position] * vector)  64.5 us
    psum x1, blocking collectives, body(): lax.psum(jnp.sum(right_side * right_side), ('gx', 'gy')) + epsilon  42.2 us
    ppermute x24, starting transfers between devices, with_halo(): lax.ppermute(lax.slice_in_dim(block, 0, width, axis=dim), axis, backward)  31 us
    dot_general x16, matrix products, accumulate(): lax.dot_general(piece, onehot, (((1,), (1,)), ((), ())), precision=lax.Pr...  27.2 us
    ppermute x24, waiting for transfers between devices, with_halo(): lax.ppermute(lax.slice_in_dim(block, block.shape[dim] - width, None, axis...  22.9 us
  transfers between devices with their start and end apart: 48, of which 23 were waited for; matrix products, arithmetic and copies ran while one was open for 1% of the time, Pallas kernels for 0%

commit v1 on v0

--- a/solution.py
+++ b/solution.py
@@ -141,7 +141,11 @@
     padded = lax.dynamic_update_slice(
         jnp.zeros((2, total_coarse), jnp.float32), partial_value, (jnp.zeros((), jnp.int32), offset)
     )
-    whole = lax.psum(padded, ("gx", "gy"))
+
+    def unite_the_leaf(xin, axis_id, chip_axis="gx"):
+        return jax.lax.psum(jax.lax.psum(xin, axis_id), chip_axis)
+
+    whole = unite_the_leaf(padded, "gy")
     own_re = jnp.dot(coarse_inverse[0], whole[0], precision=highest) - jnp.dot(
         coarse_inverse[1], whole[1], precision=highest
     )

time: 821 us -> 754 us (0.918)
  blocking collectives: 406 us -> 340 us
    psum x4 -> x8, blocking collectives: 189 us -> 130 us  [unite_the_leaf(): return jax.lax.psum(jax.lax.psum(xin, axis_id), chip_axis)]
where the time goes in v1:
time: 754 us; the launch traced here: 743 us
  blocking collectives  340 us (45%)
  other arithmetic  135 us (18%)
  starting transfers between devices  128 us (17%)
  between operations  54.6 us (7%)
  matrix products  39.1 us (5%)
  waiting for transfers between devices  23.3 us (3%)
  local copies, waits for them, and re-layouts  22.3 us (3%)
    psum x4, blocking collectives, body(): dots, squared = lax.psum((local_dots, jnp.sum(image * image)), ('gx', 'gy'))  168 us
    psum x8, blocking collectives, unite_the_leaf(): return jax.lax.psum(jax.lax.psum(xin, axis_id), chip_axis)  130 us
    ppermute x24, starting transfers between devices, with_halo(): lax.ppermute(lax.slice_in_dim(block, block.shape[dim] - width, None, axis...  97.2 us
    reduce_sum x34, other arithmetic, least_squares(): weight = jnp.sum(ortho[position] * vector)  64.5 us
    psum x1, blocking collectives, body(): lax.psum(jnp.sum(right_side * right_side), ('gx', 'gy')) + epsilon  42.2 us
    ppermute x24, starting transfers between devices, with_halo(): lax.ppermute(lax.slice_in_dim(block, 0, width, axis=dim), axis, backward)  31 us
    dot_general x16, matrix products, accumulate(): lax.dot_general(piece, onehot, (((1,), (1,)), ((), ())), precision=lax.Pr...  27.2 us
    ppermute x24, waiting for transfers between devices, with_halo(): lax.ppermute(lax.slice_in_dim(block, block.shape[dim] - width, None, axis...  23.3 us
  transfers between devices with their start and end apart: 48, of which 23 were waited for; matrix products, arithmetic and copies ran while one was open for 1% of the time, Pallas kernels for 0%

profile of v1, /device:TPU:0, one launch (start us, length us, event | category | flops | bytes accessed | tf_op | source)
XLA Modules:
  0.0 742.7 jit_solution(1943604673079011715)
XLA Ops:
  2.5 42.2 %psum.119 = f32[]{:T(128)} all-reduce(f32[]{:T(128)} %multiply_reduce_fusion.3), channel_id=1, replica_groups=mesh['gx'=4,'gy'=8] {'gx','gy'}, use_global_device_ids=true, to_apply=%region_1.0 | all-reduce | flops 1 | bytes 8 | tf_op jit(solution)/shard_map/psum | solution.py:172
  48.0 3.0 collective-permute-start.1
  53.2 5.0 collective-permute-start.3
  62.3 3.0 collective-permute-start.5
  67.5 5.4 collective-permute-start.7
  76.2 7.0 while.117
  83.3 24.4 %psum.120 = f32[2,512]{1,0:T(2,128)S(1)} all-reduce(f32[2,512]{1,0:T(2,128)S(1)} %dynamic_update_slice.40), channel_id=1, replica_groups=mesh['gx'=4,'gy'=8] {'gy'}, use_global_device_ids=true, to_apply=%region_4.0 | all-reduce | flops 1024 | bytes 8192 | tf_op jit(solution)/shard_map/psum | solution.py:146
  107.8 8.1 %psum.121 = f32[2,512]{1,0:T(2,128)S(1)} all-reduce(f32[2,512]{1,0:T(2,128)S(1)} %psum.120), channel_id=1, replica_groups=mesh['gx'=4,'gy'=8] {'gx'}, use_global_device_ids=true, to_apply=%region_5.0 | all-reduce | flops 1024 | bytes 8192 | tf_op jit(solution)/shard_map/psum | solution.py:146
  121.0 3.0 collective-permute-start.9
  126.2 4.5 collective-permute-start.11
  135.5 41.8 %all-reduce.29 = (f32[2,1]{0,1:T(1,128)S(1)}, f32[]{:T(128)}) all-reduce(f32[2,1]{0,1:T(1,128)S(1)} %maximum_bitcast_fusion.1, f32[]{:T(128)} %multiply_reduce_fusion.2), channel_id=1, replica_groups=mesh['gx'=4,'gy'=8] {'gx','gy'}, use_global_device_ids=true, to_apply=%region_10.0 | all-reduce | flops 3 | bytes 24 | tf_op jit(solution)/shard_map/psum | solution.py:185
  183.0 3.0 collective-permute-start.13
  188.2 5.0 collective-permute-start.15
  198.1 3.5 collective-permute-start.17
  204.0 5.6 collective-permute-start.19
  214.2 6.9 while.118
  221.3 24.6 %psum.124 = f32[2,512]{1,0:T(2,128)S(1)} all-reduce(f32[2,512]{1,0:T(2,128)S(1)} %dynamic_update_slice.41), channel_id=1, replica_groups=mesh['gx'=4,'gy'=8] {'gy'}, use_global_device_ids=true, to_apply=%region_16.0 | all-reduce | flops 1024 | bytes 8192 | tf_op jit(solution)/shard_map/psum | solution.py:146
  245.9 7.9 %psum.125 = f32[2,512]{1,0:T(2,128)S(1)} all-reduce(f32[2,512]{1,0:T(2,128)S(1)} %psum.124), channel_id=1, replica_groups=mesh['gx'=4,'gy'=8] {'gx'}, use_global_device_ids=true, to_apply=%region_17.0 | all-reduce | flops 1024 | bytes 8192 | tf_op jit(solution)/shard_map/psum | solution.py:146
  259.2 3.0 collective-permute-start.21
  264.4 4.5 collective-permute-start.23
  275.3 41.9 %all-reduce.28 = (f32[2,2]{0,1:T(2,128)S(1)}, f32[]{:T(128)}) all-reduce(f32[2,2]{0,1:T(2,128)S(1)} %pad_maximum_fusion.166, f32[]{:T(128)} %multiply_reduce_fusion.1), channel_id=1, replica_groups=mesh['gx'=4,'gy'=8] {'gx','gy'}, use_global_device_ids=true, to_apply=%region_24.0 | all-reduce | flops 5 | bytes 40 | tf_op jit(solution)/shard_map/psum | solution.py:185
  324.1 3.0 collective-permute-start.25
  329.3 5.0 collective-permute-start.27
  338.7 3.5 collective-permute-start.29
  344.3 5.2 collective-permute-start.31
  355.0 6.9 while.119
  362.2 24.6 %psum.128 = f32[2,512]{1,0:T(2,128)S(1)} all-reduce(f32[2,512]{1,0:T(2,128)S(1)} %dynamic_update_slice.42), channel_id=1, replica_groups=mesh['gx'=4,'gy'=8] {'gy'}, use_global_device_ids=true, to_apply=%region_30.0 | all-reduce | flops 1024 | bytes 8192 | tf_op jit(solution)/shard_map/psum | solution.py:146
  386.7 8.1 %psum.129 = f32[2,512]{1,0:T(2,128)S(1)} all-reduce(f32[2,512]{1,0:T(2,128)S(1)} %psum.128), channel_id=1, replica_groups=mesh['gx'=4,'gy'=8] {'gx'}, use_global_device_ids=true, to_apply=%region_31.0 | all-reduce | flops 1024 | bytes 8192 | tf_op jit(solution)/shard_map/psum | solution.py:146
  400.2 3.0 collective-permute-start.33
  405.4 4.5 collective-permute-start.35
  418.9 41.9 %all-reduce.27 = (f32[2,3]{0,1:T(4,128)S(1)}, f32[]{:T(128)}) all-reduce(f32[2,3]{0,1:T(4,128)S(1)} %pad_maximum_fusion.161, f32[]{:T(128)} %multiply_reduce_fusion), channel_id=1, replica_groups=mesh['gx'=4,'gy'=8] {'gx','gy'}, use_global_device_ids=true, to_apply=%region_40.0 | all-reduce | flops 7 | bytes 56 | tf_op jit(solution)/shard_map/psum | solution.py:185
  472.0 3.0 collective-permute-start.37
  477.9 5.1 collective-permute-start.39
  487.3 3.3 collective-permute-start.41
  492.8 5.2 collective-permute-start.43
  499.9 2.8 divide_subtract_fusion
  502.7 6.9 while.120
  509.8 24.7 %psum.132 = f32[2,512]{1,0:T(2,128)S(1)} all-reduce(f32[2,512]{1,0:T(2,128)S(1)} %dynamic_update_slice.43), channel_id=1, replica_groups=mesh['gx'=4,'gy'=8] {'gy'}, use_global_device_ids=true, to_apply=%region_46.0 | all-reduce | flops 1024 | bytes 8192 | tf_op jit(solution)/shard_map/psum | solution.py:146
  534.5 7.3 psum.133
  543.4 4.3 while.116
  550.5 3.0 collective-permute-start.45
  555.7 4.5 collective-permute-start.47
  570.9 42.1 %all-reduce.26 = (f32[2,4]{0,1:T(4,128)S(1)}, f32[]{:T(128)}) all-reduce(f32[2,4]{0,1:T(4,128)S(1)} %pad_maximum_fusion.162, f32[]{:T(128)} %fusion.133), channel_id=1, replica_groups=mesh['gx'=4,'gy'=8] {'gx','gy'}, use_global_device_ids=true, to_apply=%region_58.0 | all-reduce | flops 9 | bytes 72 | tf_op jit(solution)/shard_map/psum | solution.py:185
  641.8 2.6 multiply_reduce_fusion.41
  648.2 2.6 multiply_reduce_fusion.39
  659.0 3.1 multiply_reduce_fusion.29
  669.6 2.6 multiply_reduce_fusion.19
  674.0 3.1 multiply_reduce_fusion.17
  (494 shorter events, 239.6 us)
Async XLA Ops:
  46.7 4.3 collective-permute-start
  48.0 3.9 collective-permute-start.1
  51.9 6.5 collective-permute-start.2
  53.2 6.5 collective-permute-start.3
  61.0 4.3 collective-permute-start.4
  62.3 3.9 collective-permute-start.5
  66.2 7.0 collective-permute-start.6
  67.5 6.9 collective-permute-start.7
  119.7 4.3 collective-permute-start.8
  121.0 3.9 collective-permute-start.9
  124.9 6.1 collective-permute-start.10
  126.2 6.0 collective-permute-start.11
  181.7 4.3 collective-permute-start.12
  183.0 3.9 collective-permute-start.13
  186.9 6.5 collective-permute-start.14
  188.2 6.4 collective-permute-start.15
  196.9 4.8 collective-permute-start.16
  198.1 4.5 collective-permute-start.17
  202.7 7.1 collective-permute-start.18
  204.0 6.6 collective-permute-start.19
  257.9 4.3 collective-permute-start.20
  259.2 3.9 collective-permute-start.21
  263.1 6.1 collective-permute-start.22
  264.4 6.0 collective-permute-start.23
  322.8 4.3 collective-permute-start.24
  324.1 3.9 collective-permute-start.25
  328.0 6.5 collective-permute-start.26
  329.3 6.4 collective-permute-start.27
  337.4 4.8 collective-permute-start.28
  338.7 4.3 collective-permute-start.29
  343.0 6.7 collective-permute-start.30
  344.3 6.6 collective-permute-start.31
  398.9 4.4 collective-permute-start.32
  400.2 3.9 collective-permute-start.33
  404.1 6.1 collective-permute-start.34
  405.4 6.0 collective-permute-start.35
  470.7 5.8 collective-permute-start.36
  472.0 4.5 collective-permute-start.37
  476.6 6.6 collective-permute-start.38
  477.9 6.5 collective-permute-start.39
  486.0 4.8 collective-permute-start.40
  487.3 4.1 collective-permute-start.41
  491.5 6.7 collective-permute-start.42
  492.8 6.6 collective-permute-start.43
  549.2 4.4 collective-permute-start.44
  550.5 3.9 collective-permute-start.45
  554.4 6.1 collective-permute-start.46
  555.7 6.0 collective-permute-start.47
  (68 other events, 870.3 us)
